TPU v7x, 256 devices: a whole 4x4x8 slice. The times are simulated.
256 devices in a mesh: space: 64 (over z, y, core), tm: 4 (over x).
Axes of the slice: x: 4, y: 4, z: 8, core: 2. Of those that a mesh axis runs over, the one named last changes fastest.
Arguments:
- precip: float32 [512, 384, 2048], P('tm', 'space'), may hold values from 0.0001 to 0.01
Outputs:
- totals: float32 [384, 2048, 512], P(None, 'space', 'tm')
All inputs are finite; a program needn't handle non-finite values.
Results may differ from a plain program's by a relative error of at most 0.00005.
Values sent between devices are 32-bit elements; how exact they have to be, the bound alone decides.
A program may use at most 64 MiB of HBM per device.

v0:
```python
import jax
import jax.numpy as jnp
from jax import lax
from jax.sharding import Mesh
from jax.sharding import PartitionSpec as P

SPACE = ("space_0", "space_1", "space_2")


def in_blocks(value, dim, peers):
    before, after = (value.shape[:dim], value.shape[dim + 1 :])
    return jnp.moveaxis(value.reshape(*before, peers, -1, *after), dim, 0)


def joined_along(pieces, dim):
    pieces = jnp.moveaxis(pieces, 0, dim)
    dims = pieces.shape
    return pieces.reshape(*dims[:dim], dims[dim] * dims[dim + 1], *dims[dim + 2 :])


def moved_by_axis(pieces, axes, order):
    dims = [lax.axis_size(a) for a in axes]
    pieces = pieces.reshape(*dims, *pieces.shape[1:])
    for k in order:
        pieces = lax.all_to_all(pieces, axes[k], split_axis=k, concat_axis=k, tiled=True)
    return pieces.reshape(-1, *pieces.shape[len(axes) :])


def core_and_chips(value, groups, order, split_dim, concat_dim):
    peers = lax.axis_size(groups[0]) * lax.axis_size(groups[1])
    pieces = in_blocks(value, split_dim, peers)
    return joined_along(moved_by_axis(pieces, groups, order), concat_dim)


def from_everyone(value, axis):
    copies = jnp.broadcast_to(value, (lax.axis_size(axis), *value.shape))
    return lax.all_to_all(copies, axis, split_axis=0, concat_axis=0, tiled=True)


def folded_in_pairs(pieces, combine):
    while len(jax.tree.leaves(pieces)[0]) > 1:
        pieces = jax.vmap(combine)(*(pieces[side::2] for side in (0, 1)))
    return pieces[0]


def carried_in(value, axis, combine, identity):
    peers, mine = (lax.axis_size(axis), lax.axis_index(axis))
    passed = jnp.arange(peers) < mine

    def kept(part, zero, own):
        part = jnp.where(
            passed.reshape(-1, *(1 for _ in own.shape)), part, jnp.asarray(zero, own.dtype)
        )
        return part

    pieces = from_everyone(value, axis)
    return folded_in_pairs(kept(pieces, identity, value), combine)


def rechunk(source):
    return core_and_chips(source, (("space_0", "space_1"), "space_2"), (1, 0), 2, 1)


def add_terms(earlier_part, later_part):
    return earlier_part + later_part


def per_device(precip):
    day_count = precip.shape[0]
    position = lax.broadcasted_iota(jnp.int32, (day_count, day_count), 0)
    later_pos = lax.broadcasted_iota(jnp.int32, (day_count, day_count), 1)
    upper_ones = (position <= later_pos).astype(jnp.float32)
    flat_days = precip.reshape(day_count, -1)
    running = jnp.dot(
        upper_ones.T, flat_days, precision=lax.Precision.HIGHEST, preferred_element_type=jnp.float32
    )
    running = running.reshape(precip.shape)
    last_day = running[-1]
    carried = carried_in(last_day, "tm", add_terms, jnp.zeros_like(last_day))
    return jnp.transpose(rechunk(running + carried[None]), (1, 2, 0))


def solution(mesh):
    finer = Mesh(
        mesh.devices.reshape(8, 4, 2, mesh.shape["tm"]), ("space_0", "space_1", "space_2", "tm")
    )
    placed = (P("tm", SPACE, None),)
    return jax.shard_map(
        per_device, mesh=finer, in_specs=placed, out_specs=P(None, SPACE, "tm"), check_vma=False
    )
```

profile of v0, /device:TPU:1, one launch (start us, length us, event | category | flops | bytes accessed | tf_op | source)
XLA Modules:
  0.0 196.2 jit_solution(15107310221342891865)
XLA Ops:
  0.0 6.6 %copy.10 = f32[128,6,2048]{0,2,1:T(8,128)} copy(f32[128,6,2048]{2,0,1:T(8,128)} %param.1) | data formatting | bytes 12582912 | tf_op args[0]
  6.6 5.3 %fusion.1 = f32[128,12288]{1,0:T(8,128)S(1)} fusion(f32[128,12288]{0,1:T(8,128)} %bitcast.15), kind=kOutput, calls=%fused_computation.7 | convolution fusion | flops 2415951872 | bytes 12582912 | tf_op jit(solution)/shard_map/dot_general | solution.py:74
  11.9 0.0 copy-start
  11.9 2.7 %copy-done = f32[128,12288]{1,0:T(8,128)} copy-done((f32[128,12288]{1,0:T(8,128)}, f32[128,12288]{1,0:T(8,128)S(1)}, u32[]{:S(2)}) %copy-start) | copy-done | bytes 6291480
  14.6 0.1 slice_reduce_fusion
  14.7 0.7 broadcast_in_dim.17
  15.5 4.8 %all-to-all-start = ((f32[4,6,2048]{2,1,0:T(8,128)}), f32[4,6,2048]{2,1,0:T(8,128)S(1)}, u32[]{:S(2)}, u32[]{:S(2)}) async-start(f32[4,6,2048]{2,1,0:T(8,128)} %broadcast_in_dim.17), calls=%async_computation | async-start | bytes 524288 | tf_op jit(solution)/shard_map/all_to_all | solution.py:37
  20.3 6.6 %copy.11 = f32[128,12288]{0,1:T(8,128)} copy(f32[128,12288]{1,0:T(8,128)} %copy-done) | data formatting | bytes 12582912 | tf_op jit(solution)/shard_map/dot_general | solution.py:74
  26.9 0.0 all-to-all-done
  26.9 0.1 broadcast_select_fusion
  27.0 0.1 add.19
  27.1 4.4 %broadcast_add_fusion = f32[128,6,64,32]{0,3,2,1:T(8,128)S(1)} fusion(f32[128,6,64,32]{0,3,2,1:T(8,128)} %bitcast.13, f32[6,64,32]{2,1,0:T(8,128)S(1)} %add.19), kind=kLoop, calls=%fused_computation | loop fusion | flops 1572864 | bytes 12632064 | tf_op jit(solution)/shard_map/add | solution.py:80
  31.6 1.0 copy.12
  32.6 10.2 %all_to_all.15 = f32[32,2,128,6,32]{2,4,0,3,1:T(8,128)S(1)} all-to-all(f32[32,2,128,6,32]{2,4,0,3,1:T(8,128)S(1)} %copy.12), channel_id=1, replica_groups=mesh['space_0'=8,'space_1'=4,'space_2'=2,'tm'=4] {'space_2'}, dimensions={1} | all-to-all | bytes 12582912 | tf_op jit(solution)/shard_map/all_to_all | solution.py:25
  42.8 1.0 copy.13
  43.9 148.9 %all_to_all.16 = f32[32,2,128,6,32]{2,4,1,3,0:T(8,128)S(1)} all-to-all(f32[32,2,128,6,32]{2,4,1,3,0:T(8,128)S(1)} %copy.13), channel_id=1, replica_groups=mesh['space_0'=8,'space_1'=4,'space_2'=2,'tm'=4] {'space_0','space_1'}, dimensions={0} | all-to-all | bytes 12582912 | tf_op jit(solution)/shard_map/all_to_all | solution.py:25
  192.8 3.4 %copy.14 = f32[32,2,128,6,32]{2,4,3,1,0:T(8,128)} copy(f32[32,2,128,6,32]{2,4,1,3,0:T(8,128)S(1)} %all_to_all.16) | data formatting | bytes 12582912 | tf_op jit(solution)/shard_map/all_to_all | solution.py:25
  (4 shorter events, 0.0 us)
Async XLA Ops:
  11.9 2.7 %copy-start = (f32[128,12288]{1,0:T(8,128)}, f32[128,12288]{1,0:T(8,128)S(1)}, u32[]{:S(2)}) copy-start(f32[128,12288]{1,0:T(8,128)S(1)} %fusion.1) | copy-start | bytes 18874372
  15.5 11.4 %all-to-all-start = ((f32[4,6,2048]{2,1,0:T(8,128)}), f32[4,6,2048]{2,1,0:T(8,128)S(1)}, u32[]{:S(2)}, u32[]{:S(2)}) async-start(f32[4,6,2048]{2,1,0:T(8,128)} %broadcast_in_dim.17), calls=%async_computation | async-start | bytes 524288 | tf_op jit(solution)/shard_map/all_to_all | solution.py:37
where the time goes:
time: 198 us; the launch traced here: 196 us
  blocking collectives  159 us (80%)
  local copies, waits for them, and re-layouts  22.3 us (11%)
  matrix products  5.31 us (3%)
  starting transfers between devices  4.83 us (2%)
  other arithmetic  4.54 us (2%)
    all_to_all x2, blocking collectives, moved_by_axis(): lax.all_to_all(pieces, axes[k], split_axis=k, concat_axis=k, tiled=True)  159 us
    unnamed x3, local copies, waits for them, and re-layouts  9.25 us
    dot_general x1, local copies, waits for them, and re-layouts, per_device(): jnp.dot(upper_ones.T, flat_days, precision=lax.Precision.HIGHEST, preferr...  6.59 us
    dot_general x1, matrix products, per_device(): jnp.dot(upper_ones.T, flat_days, precision=lax.Precision.HIGHEST, preferr...  5.31 us
    all_to_all x1, starting transfers between devices, from_everyone(): return lax.all_to_all(copies, axis, split_axis=0, concat_axis=0, tiled=True)  4.83 us
    all_to_all x2, local copies, waits for them, and re-layouts, moved_by_axis(): lax.all_to_all(pieces, axes[k], split_axis=k, concat_axis=k, tiled=True)  4.45 us
    add x1, other arithmetic, per_device(): return jnp.transpose(rechunk(running + carried[None]), (1, 2, 0))  4.42 us
  transfers between devices with their start and end apart: 1, of which 0 were waited for; matrix products, arithmetic and copies ran while one was open for 3% of the time, Pallas kernels for 0%

commit v1 on v0

v1 whole, which is shorter than its diff:
```python
import functools

import jax
import jax.numpy as jnp
from jax import lax
from jax.experimental import pallas as pl
from jax.experimental.pallas import tpu as pltpu
from jax.sharding import PartitionSpec as P

MESH = pl.DeviceIdType.MESH
Z, Y, C, X = 8, 4, 2, 4
ROWS, DAYS, COLS = 6, 128, 32
WIDE = Y * C * COLS
HOPS = [4, 3, 5, 2, 6, 1, 7, 0]
SIDE = [(2, 1), (2, 0), (1, 0), (3, 0), (1, 1), (3, 1), (0, 1)]


def kernel(x_ref, out_ref, inp, stage, relay, sums, earlier, load_sem,
           xs_sem, xr_sem, ys_sem, yr_sem, zs_sem, zr_sem):
    me = lax.axis_index("space")
    t = lax.axis_index("tm")
    z, yc = me // (Y * C), lax.rem(me, Y * C)
    y, c = yc // C, lax.rem(yc, C)

    def side(dy, dc):
        return lax.rem(y + dy, Y) * C + lax.rem(c + dc, C)

    zs = [lax.rem(z + d, Z) for d in HOPS]
    to = [side(dy, dc) for dy, dc in SIDE]
    source = [side(Y - dy, C - dc) for dy, dc in SIDE]

    loads = []
    for i in range(Z):
        cp = pltpu.make_async_copy(
            x_ref.at[:, :, pl.ds(pl.multiple_of(zs[i] * WIDE, WIDE), WIDE)], inp.at[i], load_sem.at[i])
        cp.start()
        loads.append(cp)

    barrier = pltpu.get_barrier_semaphore()
    for i in range(Z - 1):
        pl.semaphore_signal(barrier, inc=1, device_id={"space": zs[i] * Y * C + yc}, device_id_type=MESH)
    for k in to:
        pl.semaphore_signal(barrier, inc=1, device_id={"space": z * Y * C + k}, device_id_type=MESH)
    for d in range(1, X):
        pl.semaphore_signal(barrier, inc=1, device_id={"tm": lax.rem(t + d, X)}, device_id_type=MESH)

    def add_days(i):
        def row(r, _):
            sums[i, pl.ds(r, 1), :] = jnp.sum(inp[i, r], axis=0, keepdims=True)
            return 0
        lax.fori_loop(0, ROWS, row, 0)

    trades = [[] for _ in range(Z)]
    for i in range(Z):
        loads[i].wait()
        add_days(i)
        if i == 0:
            pl.semaphore_wait(barrier, (Z - 1) + len(SIDE) + (X - 1))
        for d in range(1, X):
            cp = pltpu.make_async_remote_copy(
                sums.at[i], earlier.at[d - 1, i], xs_sem.at[d - 1, i], xr_sem.at[d - 1, i],
                device_id={"tm": lax.rem(t + d, X)}, device_id_type=MESH)
            cp.start()
            trades[i].append(cp)

    lower = (lax.broadcasted_iota(jnp.int32, (DAYS, DAYS), 0)
             >= lax.broadcasted_iota(jnp.int32, (DAYS, DAYS), 1)).astype(jnp.bfloat16)

    def dot(part):
        return jnp.dot(lower, part, preferred_element_type=jnp.float32)

    def totals(i):
        def row(r, _):
            value = inp[i, r]
            high = value.astype(jnp.bfloat16)
            rest = value - high.astype(jnp.float32)
            mid = rest.astype(jnp.bfloat16)
            low = (rest - mid.astype(jnp.float32)).astype(jnp.bfloat16)
            running = dot(low) + dot(mid) + dot(high)
            before = jnp.zeros((1, WIDE), jnp.float32)
            for d in range(1, X):
                got = earlier[d - 1, i, pl.ds(r, 1), :]
                before = before + jnp.where(t >= d, got, jnp.zeros_like(got))
            stage[:, i, r] = (running + before).T.reshape(Y * C, COLS, DAYS)
            return 0
        lax.fori_loop(0, ROWS, row, 0)

    direct, across = [None] * Z, [[None] * len(SIDE) for _ in range(Z)]
    for i in range(Z):
        for cp in trades[i]:
            cp.wait_recv()
        totals(i)
        if HOPS[i]:
            direct[i] = pltpu.make_async_remote_copy(
                stage.at[yc, i], out_ref.at[z, yc], zs_sem.at[i, len(SIDE)], zr_sem.at[i, len(SIDE)],
                device_id={"space": zs[i] * Y * C + yc}, device_id_type=MESH)
            direct[i].start()
        else:
            out_ref[z, yc] = stage[yc, i]
        for j, k in enumerate(to):
            landing = relay.at[j, i] if HOPS[i] else out_ref.at[z, yc]
            across[i][j] = pltpu.make_async_remote_copy(
                stage.at[k, i], landing, ys_sem.at[j, i], yr_sem.at[j, i],
                device_id={"space": z * Y * C + k}, device_id_type=MESH)
            across[i][j].start()

    onward = []
    for i in range(Z):
        for j in range(len(SIDE)):
            across[i][j].wait_recv()
            if HOPS[i]:
                cp = pltpu.make_async_remote_copy(
                    relay.at[j, i], out_ref.at[z, source[j]], zs_sem.at[i, j], zr_sem.at[i, j],
                    device_id={"space": zs[i] * Y * C + yc}, device_id_type=MESH)
                cp.start()
                onward.append(cp)

    for i in range(Z):
        for cp in trades[i] + across[i]:
            cp.wait_send()
    for cp in direct[:-1] + onward:
        cp.wait()


def per_device(precip):
    rows_first = jnp.transpose(precip, (1, 0, 2))
    side = len(SIDE)
    out = pl.pallas_call(
        kernel,
        name="rechunk",
        out_shape=jax.ShapeDtypeStruct((Z, Y * C, ROWS, COLS, DAYS), jnp.float32),
        in_specs=[pl.BlockSpec(memory_space=pltpu.HBM)],
        out_specs=pl.BlockSpec(memory_space=pltpu.VMEM),
        scratch_shapes=[
            pltpu.VMEM((Z, ROWS, DAYS, WIDE), jnp.float32),
            pltpu.VMEM((Y * C, Z, ROWS, COLS, DAYS), jnp.float32),
            pltpu.VMEM((side, Z - 1, ROWS, COLS, DAYS), jnp.float32),
            pltpu.VMEM((Z, ROWS, WIDE), jnp.float32),
            pltpu.VMEM((X - 1, Z, ROWS, WIDE), jnp.float32),
            pltpu.SemaphoreType.DMA((Z,)),
            pltpu.SemaphoreType.DMA((X - 1, Z)),
            pltpu.SemaphoreType.DMA((X - 1, Z)),
            pltpu.SemaphoreType.DMA((side, Z)),
            pltpu.SemaphoreType.DMA((side, Z)),
            pltpu.SemaphoreType.DMA((Z, side + 1)),
            pltpu.SemaphoreType.DMA((Z, side + 1)),
        ],
        compiler_params=pltpu.CompilerParams(
            collective_id=0, has_side_effects=True, vmem_limit_bytes=46 * 2**20),
    )(rows_first)
    return out.reshape(Z * Y * C * ROWS, COLS, DAYS)


def solution(mesh):
    return jax.shard_map(
        per_device, mesh=mesh, in_specs=(P("tm", "space", None),),
        out_specs=P(None, "space", "tm"), check_vma=False)
```

time: 198 us -> 157 us (0.79); the launches traced: 196 us -> 157 us
  blocking collectives: 159 us -> 0 us
  Pallas kernels: 0 us -> 155 us
  local copies, waits for them, and re-layouts: 22.3 us -> 2.71 us
  matrix products: 5.31 us -> 0 us
  starting transfers between devices: 4.83 us -> 0 us
  other arithmetic: 4.54 us -> 0 us
    all_to_all x2 -> x0, blocking collectives: 159 us -> none  [moved_by_axis(): lax.all_to_all(pieces, axes[k], split_axis=k, concat_axis=k, tiled=True)]
    pallas_call x0 -> x1, Pallas kernels: none -> 155 us  [per_device(): pl.pallas_call(kernel, name='rechunk', out_shape=jax.ShapeDtypeStruct((Z,...]
    dot_general x1 -> x0, local copies, waits for them, and re-layouts: 6.59 us -> none  [per_device(): jnp.dot(upper_ones.T, flat_days, precision=lax.Precision.HIGHEST, preferr...]
    unnamed x3 -> x1, local copies, waits for them, and re-layouts: 9.25 us -> 2.71 us
    dot_general x1 -> x0, matrix products: 5.31 us -> none  [per_device(): jnp.dot(upper_ones.T, flat_days, precision=lax.Precision.HIGHEST, preferr...]
    all_to_all x1 -> x0, starting transfers between devices: 4.83 us -> none  [from_everyone(): return lax.all_to_all(copies, axis, split_axis=0, concat_axis=0, tiled=True)]
    all_to_all x2 -> x0, local copies, waits for them, and re-layouts: 4.45 us -> none  [moved_by_axis(): lax.all_to_all(pieces, axes[k], split_axis=k, concat_axis=k, tiled=True)]
    add x3 -> x0, other arithmetic: 4.44 us -> none  [the longest x1 4.42 us: per_device(): return jnp.transpose(rechunk(running + carried[None]), (1, 2, 0))]
  transfers between devices with their start and end apart: 1 -> 0, of which waited for: 0 -> 0; matrix products, arithmetic and copies ran while one was open for 3% -> 0% of each run, Pallas kernels for 0% -> 0%
where the time goes in v1:
time: 157 us
  Pallas kernels  155 us (99%)
  local copies, waits for them, and re-layouts  2.71 us (2%)
    pallas_call x1, Pallas kernels, per_device(): pl.pallas_call(kernel, name='rechunk', out_shape=jax.ShapeDtypeStruct((Z,...  155 us

profile of v1, /device:TPU:1, one launch (start us, length us, event | category | flops | bytes accessed | tf_op | source)
XLA Modules:
  0.0 157.4 jit_solution(850922445038761756)
XLA Ops:
  0.0 154.6 %rechunk.1 = f32[8,8,6,32,128]{4,3,2,1,0:T(8,128)S(1)} custom-call(f32[6,128,2048]{2,1,0:T(8,128)} %bitcast.3), custom_call_target="tpu_custom_call" | custom-call | tf_op jit(solution)/shard_map/rechunk/pallas_call | solution.py:128
  154.7 2.7 %copy.3 = f32[384,32,128]{2,1,0:T(8,128)} copy(f32[384,32,128]{2,1,0:T(8,128)S(1)} %bitcast.2) | data formatting | bytes 12582912

commit v2 on v1

v2 whole, which is shorter than its diff:
```python
import jax
import jax.numpy as jnp
from jax import lax
from jax.experimental import pallas as pl
from jax.experimental.pallas import tpu as pltpu
from jax.sharding import PartitionSpec as P

MESH = pl.DeviceIdType.MESH
Z, Y, C, X = 8, 4, 2, 4
ROWS, DAYS, COLS, LANES = 6, 128, 32, 128
WIDE = Y * C * COLS
HOPS = [4, 3, 5, 2, 6, 1, 7, 0]
EARLY = 3
WAVES = [(1, 2), (3, 4), (0,), (5, 6), (7,)]
ORDER = [i for wave in WAVES for i in wave]
SIDE = [(2, 1), (2, 0), (1, 0), (3, 0), (1, 1), (3, 1), (0, 1)]
S = len(SIDE)
FINE = 1
UNROLL = 3


def kernel(x_ref, out_ref, inp, stage, relay, first, sums, earlier, late, late_in, column,
           ahead_sem, load_sem, xs_sem, xr_sem, ys_sem, fine_sem, wave_sem, zs_sem, early_sem, direct_sem, onward_sem,
           ls_sem, lr_sem):
    me = lax.axis_index("space")
    t = lax.axis_index("tm")
    z, yc = me // (Y * C), lax.rem(me, Y * C)
    y, c = yc // C, lax.rem(yc, C)

    def side(dy, dc):
        return lax.rem(y + dy, Y) * C + lax.rem(c + dc, C)

    zs = [lax.rem(z + d, Z) for d in HOPS]
    to = [side(dy, dc) for dy, dc in SIDE]
    source = [side(Y - dy, C - dc) for dy, dc in SIDE]
    half = pl.multiple_of(yc // C // 2 * LANES, LANES)
    within = pl.multiple_of(lax.rem(yc, LANES // COLS) * COLS, COLS)

    def load(i, start, width, sem):
        pltpu.make_async_copy(
            x_ref.at[:, :, pl.ds(pl.multiple_of(zs[i] * WIDE + start, LANES), width)],
            inp.at[i, :, :, pl.ds(start, width)], sem).start()

    for i in range(EARLY):
        load(i, half, LANES, ahead_sem.at[i])
    for i in range(Z):
        if i < EARLY:
            load(i, pl.multiple_of(LANES - half, LANES), LANES, load_sem)
        else:
            load(i, 0, WIDE, load_sem)

    barrier = pltpu.get_barrier_semaphore()
    for i in range(Z - 1):
        pl.semaphore_signal(barrier, inc=1, device_id={"space": zs[i] * Y * C + yc}, device_id_type=MESH)
    for k in to:
        pl.semaphore_signal(barrier, inc=1, device_id={"space": z * Y * C + k}, device_id_type=MESH)
    for d in range(1, X):
        pl.semaphore_signal(barrier, inc=1, device_id={"tm": lax.rem(t + d, X)}, device_id_type=MESH)

    lower = (lax.broadcasted_iota(jnp.int32, (DAYS, DAYS), 0)
             >= lax.broadcasted_iota(jnp.int32, (DAYS, DAYS), 1)).astype(jnp.bfloat16)

    def dot(part):
        return jnp.dot(lower, part, preferred_element_type=jnp.float32)

    def over_days(value):
        high = value.astype(jnp.bfloat16)
        rest = value - high.astype(jnp.float32)
        mid = rest.astype(jnp.bfloat16)
        low = (rest - mid.astype(jnp.float32)).astype(jnp.bfloat16)
        return dot(low) + dot(mid) + dot(high)

    def each_row(body, unroll):
        def step(r, carry):
            body(r)
            return carry
        lax.fori_loop(0, ROWS, step, 0, unroll=unroll)

    def own_block(i):
        def row(r):
            first[i, r] = over_days(inp[i, r, :, pl.ds(half, LANES)]).T
        each_row(row, ROWS)

    def add_days(i):
        def row(r):
            sums[i, pl.ds(r, 1), :] = jnp.sum(inp[i, r], axis=0, keepdims=True)
        each_row(row, 1)

    def before(i, rows):
        total = jnp.zeros((1, WIDE), jnp.float32)
        for d in range(1, X):
            got = earlier[d - 1, i, rows, :]
            total = total + jnp.where(t >= d, got, jnp.zeros_like(got))
        return total

    def totals(i):
        def row(r):
            running = over_days(inp[i, r]) + before(i, pl.ds(r, 1))
            stage[:, i, r] = running.T.reshape(Y * C, COLS, DAYS)
        each_row(row, UNROLL)

    def send(src, dst, send_sem, recv_sem, **device):
        pltpu.make_async_remote_copy(
            src, dst, send_sem, recv_sem, device_id=device, device_id_type=MESH).start()

    def arrived(ref, sem):
        pltpu.make_async_remote_copy(ref, ref, sem, sem, device_id={"space": me}, device_id_type=MESH).wait_recv()

    def along_z(i):
        return zs[i] * Y * C + yc

    for i in range(EARLY):
        arrived(inp.at[i, :, :, 0:LANES], ahead_sem.at[i])
        own_block(i)
        if i == 0:
            pl.semaphore_wait(barrier, (Z - 1) + S + (X - 1))
        send(first.at[i, :, pl.ds(within, COLS), :], out_ref.at[z, yc], zs_sem, early_sem.at[i], space=along_z(i))

    arrived(x_ref.at[:, :, 0:(2 * Z - EARLY) * LANES], load_sem)
    for i in ORDER:
        add_days(i)
        for d in range(1, X):
            send(sums.at[i], earlier.at[d - 1, i], xs_sem, xr_sem.at[i], tm=lax.rem(t + d, X))

    for w, wave in enumerate(WAVES):
        for i in wave:
            arrived(earlier.at[:, i], xr_sem.at[i])
            if i < EARLY:
                total = before(i, slice(0, ROWS))
                late[i] = jnp.zeros((8, LANES), jnp.float32)
                late[i, 0:ROWS] = jnp.where(half == 0, total[:, :LANES], total[:, LANES:])
            totals(i)
            if i < EARLY:
                send(late.at[i], late_in.at[i], ls_sem, lr_sem.at[i], space=along_z(i))
            elif HOPS[i]:
                send(stage.at[yc, i], out_ref.at[z, yc], zs_sem, direct_sem, space=along_z(i))
            else:
                out_ref[z, yc] = stage[yc, i]
        for j, k in enumerate(to):
            sem = fine_sem.at[w, j] if w < FINE else wave_sem.at[w - FINE]
            for i in wave:
                landing = relay.at[j, i] if HOPS[i] else out_ref.at[z, yc]
                send(stage.at[k, i], landing, ys_sem, sem, space=z * Y * C + k)

    for w, wave in enumerate(WAVES):
        if w >= FINE:
            arrived(stage.at[0:S, 0:len(wave)], wave_sem.at[w - FINE])
        for j in range(S):
            if w < FINE:
                arrived(stage.at[0, 0:len(wave)], fine_sem.at[w, j])
            for i in wave:
                if HOPS[i]:
                    send(relay.at[j, i], out_ref.at[z, source[j]], zs_sem, onward_sem, space=along_z(i))

    for i in range(EARLY):
        arrived(stage.at[0, 0], early_sem.at[i])
        arrived(late_in.at[i], lr_sem.at[i])
        column[i] = late_in[i].T
        origin = lax.rem(z + Z - HOPS[i], Z)
        for r in range(ROWS):
            out_ref[origin, yc, r] += column[i, pl.ds(within, COLS), r:r + 1]

    arrived(earlier, xs_sem)
    arrived(late, ls_sem)
    arrived(stage.at[0:S], ys_sem)
    arrived(stage.at[0, 0:Z - 1 - EARLY], direct_sem)
    arrived(stage.at[0:Z - 1], zs_sem)
    arrived(relay, onward_sem)


def per_device(precip):
    block = (ROWS, COLS, DAYS)
    out = pl.pallas_call(
        kernel,
        name="rechunk",
        out_shape=jax.ShapeDtypeStruct((Z, Y * C, *block), jnp.float32),
        in_specs=[pl.BlockSpec(memory_space=pl.ANY)],
        out_specs=pl.BlockSpec(memory_space=pltpu.VMEM),
        scratch_shapes=[
            pltpu.VMEM((Z, ROWS, DAYS, WIDE), jnp.float32),
            pltpu.VMEM((Y * C, Z, *block), jnp.float32),
            pltpu.VMEM((S, Z - 1, *block), jnp.float32),
            pltpu.VMEM((EARLY, ROWS, LANES, DAYS), jnp.float32),
            pltpu.VMEM((Z, ROWS, WIDE), jnp.float32),
            pltpu.VMEM((X - 1, Z, ROWS, WIDE), jnp.float32),
            pltpu.VMEM((EARLY, 8, LANES), jnp.float32),
            pltpu.VMEM((EARLY, 8, LANES), jnp.float32),
            pltpu.VMEM((EARLY, LANES, 8), jnp.float32),
            pltpu.SemaphoreType.DMA((EARLY,)),
            pltpu.SemaphoreType.DMA,
            pltpu.SemaphoreType.DMA,
            pltpu.SemaphoreType.DMA((Z,)),
            pltpu.SemaphoreType.DMA,
            pltpu.SemaphoreType.DMA((FINE, S)),
            pltpu.SemaphoreType.DMA((len(WAVES) - FINE,)),
            pltpu.SemaphoreType.DMA,
            pltpu.SemaphoreType.DMA((EARLY,)),
            pltpu.SemaphoreType.DMA,
            pltpu.SemaphoreType.DMA,
            pltpu.SemaphoreType.DMA,
            pltpu.SemaphoreType.DMA((EARLY,)),
        ],
        compiler_params=pltpu.CompilerParams(
            collective_id=0, has_side_effects=True, vmem_limit_bytes=46 * 2**20),
    )(jnp.transpose(precip, (1, 0, 2)))
    return out.reshape(Z * Y * C * ROWS, COLS, DAYS)


def solution(mesh):
    return jax.shard_map(
        per_device, mesh=mesh, in_specs=(P("tm", "space", None),),
        out_specs=P(None, "space", "tm"), check_vma=False)
```

time: 157 us -> 150 us (0.955)
  Pallas kernels: 155 us -> 147 us
    pallas_call x1, Pallas kernels: 155 us -> 147 us  [per_device(): pl.pallas_call(kernel, name='rechunk', out_shape=jax.ShapeDtypeStruct((Z,...]
where the time goes in v2:
time: 150 us
  Pallas kernels  147 us (98%)
  local copies, waits for them, and re-layouts  2.71 us (2%)
    pallas_call x1, Pallas kernels, per_device(): pl.pallas_call(kernel, name='rechunk', out_shape=jax.ShapeDtypeStruct((Z,...  147 us

profile of v2, /device:TPU:1, one launch (start us, length us, event | category | flops | bytes accessed | tf_op | source)
XLA Modules:
  0.0 149.7 jit_solution(7362113368934814320)
XLA Ops:
  0.0 147.0 %rechunk.1 = f32[8,8,6,32,128]{4,3,2,1,0:T(8,128)S(1)} custom-call(f32[6,128,2048]{2,1,0:T(8,128)} %bitcast.3), custom_call_target="tpu_custom_call" | custom-call | tf_op jit(solution)/shard_map/rechunk/pallas_call | solution.py:173
  147.0 2.7 %copy.3 = f32[384,32,128]{2,1,0:T(8,128)} copy(f32[384,32,128]{2,1,0:T(8,128)S(1)} %bitcast.2) | data formatting | bytes 12582912

commit v3 on v2

--- a/solution.py
+++ b/solution.py
@@ -9,9 +9,9 @@
 Z, Y, C, X = 8, 4, 2, 4
 ROWS, DAYS, COLS, LANES = 6, 128, 32, 128
 WIDE = Y * C * COLS
-HOPS = [4, 3, 5, 2, 6, 1, 7, 0]
-EARLY = 3
-WAVES = [(1, 2), (3, 4), (0,), (5, 6), (7,)]
+HOPS = [1, 7, 2, 6, 3, 5, 4, 0]
+EARLY = 4
+WAVES = [(4, 5), (6,), (2, 3), (0, 1), (7,)]
 ORDER = [i for wave in WAVES for i in wave]
 SIDE = [(2, 1), (2, 0), (1, 0), (3, 0), (1, 1), (3, 1), (0, 1)]
 S = len(SIDE)
@@ -21,7 +21,7 @@
 
 def kernel(x_ref, out_ref, inp, stage, relay, first, sums, earlier, late, late_in, column,
            ahead_sem, load_sem, xs_sem, xr_sem, ys_sem, fine_sem, wave_sem, zs_sem, early_sem, direct_sem, onward_sem,
-           ls_sem, lr_sem):
+           ls_sem, lr_sem, seen, beside, core_seen, days_seen):
     me = lax.axis_index("space")
     t = lax.axis_index("tm")
     z, yc = me // (Y * C), lax.rem(me, Y * C)
@@ -49,13 +49,16 @@
         else:
             load(i, 0, WIDE, load_sem)
 
+    def tell(sem, **device):
+        pl.semaphore_signal(sem, inc=1, device_id=device, device_id_type=MESH)
+
+    up, down = (lax.rem(z + d, Z) * Y * C + yc for d in (1, Z - 1))
+    left, right, partner = (z * Y * C + side(dy, dc) for dy, dc in ((1, 0), (Y - 1, 0), (0, 1)))
     barrier = pltpu.get_barrier_semaphore()
-    for i in range(Z - 1):
-        pl.semaphore_signal(barrier, inc=1, device_id={"space": zs[i] * Y * C + yc}, device_id_type=MESH)
-    for k in to:
-        pl.semaphore_signal(barrier, inc=1, device_id={"space": z * Y * C + k}, device_id_type=MESH)
-    for d in range(1, X):
-        pl.semaphore_signal(barrier, inc=1, device_id={"tm": lax.rem(t + d, X)}, device_id_type=MESH)
+    for k in (up, down, left, right, partner):
+        tell(barrier, space=k)
+    for d in (1, X - 1):
+        tell(barrier, tm=lax.rem(t + d, X))
 
     lower = (lax.broadcasted_iota(jnp.int32, (DAYS, DAYS), 0)
              >= lax.broadcasted_iota(jnp.int32, (DAYS, DAYS), 1)).astype(jnp.bfloat16)
@@ -113,8 +116,25 @@
         arrived(inp.at[i, :, :, 0:LANES], ahead_sem.at[i])
         own_block(i)
         if i == 0:
-            pl.semaphore_wait(barrier, (Z - 1) + S + (X - 1))
+            pl.semaphore_wait(barrier, 7)
+            tell(seen.at[0], space=down)
+            tell(seen.at[1], space=up)
+            tell(beside, space=left)
+            tell(beside, space=right)
+            tell(days_seen, tm=lax.rem(t + X - 1, X))
+        if i == 2:
+            pl.semaphore_wait(seen.at[0], 1)
+            tell(seen.at[2], space=down)
+        if i == 3:
+            pl.semaphore_wait(seen.at[1], 1)
+            tell(seen.at[3], space=up)
         send(first.at[i, :, pl.ds(within, COLS), :], out_ref.at[z, yc], zs_sem, early_sem.at[i], space=along_z(i))
+
+    pl.semaphore_wait(seen.at[2], 1)
+    tell(seen.at[4], space=down)
+    pl.semaphore_wait(beside, 2)
+    tell(core_seen, space=partner)
+    pl.semaphore_wait(days_seen, 1)
 
     arrived(x_ref.at[:, :, 0:(2 * Z - EARLY) * LANES], load_sem)
     for i in ORDER:
@@ -122,6 +142,9 @@
         for d in range(1, X):
             send(sums.at[i], earlier.at[d - 1, i], xs_sem, xr_sem.at[i], tm=lax.rem(t + d, X))
 
+    pl.semaphore_wait(seen.at[3], 1)
+    pl.semaphore_wait(seen.at[4], 1)
+    pl.semaphore_wait(core_seen, 1)
     for w, wave in enumerate(WAVES):
         for i in wave:
             arrived(earlier.at[:, i], xr_sem.at[i])
@@ -199,6 +222,10 @@
             pltpu.SemaphoreType.DMA,
             pltpu.SemaphoreType.DMA,
             pltpu.SemaphoreType.DMA((EARLY,)),
+            pltpu.SemaphoreType.REGULAR((5,)),
+            pltpu.SemaphoreType.REGULAR,
+            pltpu.SemaphoreType.REGULAR,
+            pltpu.SemaphoreType.REGULAR,
         ],
         compiler_params=pltpu.CompilerParams(
             collective_id=0, has_side_effects=True, vmem_limit_bytes=46 * 2**20),

time: 150 us -> 149 us (level)
  no operation moved by 1% of the time
where the time goes in v3:
time: 149 us
  Pallas kernels  146 us (98%)
  local copies, waits for them, and re-layouts  2.71 us (2%)
    pallas_call x1, Pallas kernels, per_device(): pl.pallas_call(kernel, name='rechunk', out_shape=jax.ShapeDtypeStruct((Z,...  146 us

profile of v3, /device:TPU:1, one launch (start us, length us, event | category | flops | bytes accessed | tf_op | source)
XLA Modules:
  0.0 148.8 jit_solution(14215399188145568595)
XLA Ops:
  0.0 146.1 %rechunk.1 = f32[8,8,6,32,128]{4,3,2,1,0:T(8,128)S(1)} custom-call(f32[6,128,2048]{2,1,0:T(8,128)} %bitcast.3), custom_call_target="tpu_custom_call" | custom-call | tf_op jit(solution)/shard_map/rechunk/pallas_call | solution.py:196
  146.1 2.7 %copy.3 = f32[384,32,128]{2,1,0:T(8,128)} copy(f32[384,32,128]{2,1,0:T(8,128)S(1)} %bitcast.2) | data formatting | bytes 12582912

commit v4 on v3

--- a/solution.py
+++ b/solution.py
@@ -16,7 +16,7 @@
 SIDE = [(2, 1), (2, 0), (1, 0), (3, 0), (1, 1), (3, 1), (0, 1)]
 S = len(SIDE)
 FINE = 1
-UNROLL = 3
+UNROLL = 6
 
 
 def kernel(x_ref, out_ref, inp, stage, relay, first, sums, earlier, late, late_in, column,
@@ -41,6 +41,17 @@
             x_ref.at[:, :, pl.ds(pl.multiple_of(zs[i] * WIDE + start, LANES), width)],
             inp.at[i, :, :, pl.ds(start, width)], sem).start()
 
+    def tell(sem, **device):
+        pl.semaphore_signal(sem, inc=1, device_id=device, device_id_type=MESH)
+
+    up, down = (lax.rem(z + d, Z) * Y * C + yc for d in (1, Z - 1))
+    left, right, partner = (z * Y * C + side(dy, dc) for dy, dc in ((1, 0), (Y - 1, 0), (0, 1)))
+    barrier = pltpu.get_barrier_semaphore()
+    for k in (up, down, left, right, partner):
+        tell(barrier, space=k)
+    for d in (1, X - 1):
+        tell(barrier, tm=lax.rem(t + d, X))
+
     for i in range(EARLY):
         load(i, half, LANES, ahead_sem.at[i])
     for i in range(Z):
@@ -48,17 +59,6 @@
             load(i, pl.multiple_of(LANES - half, LANES), LANES, load_sem)
         else:
             load(i, 0, WIDE, load_sem)
-
-    def tell(sem, **device):
-        pl.semaphore_signal(sem, inc=1, device_id=device, device_id_type=MESH)
-
-    up, down = (lax.rem(z + d, Z) * Y * C + yc for d in (1, Z - 1))
-    left, right, partner = (z * Y * C + side(dy, dc) for dy, dc in ((1, 0), (Y - 1, 0), (0, 1)))
-    barrier = pltpu.get_barrier_semaphore()
-    for k in (up, down, left, right, partner):
-        tell(barrier, space=k)
-    for d in (1, X - 1):
-        tell(barrier, tm=lax.rem(t + d, X))
 
     lower = (lax.broadcasted_iota(jnp.int32, (DAYS, DAYS), 0)
              >= lax.broadcasted_iota(jnp.int32, (DAYS, DAYS), 1)).astype(jnp.bfloat16)

time: 149 us -> 149 us (level)
  no operation moved by 1% of the time
where the time goes in v4:
time: 149 us
  Pallas kernels  146 us (98%)
  local copies, waits for them, and re-layouts  2.71 us (2%)
    pallas_call x1, Pallas kernels, per_device(): pl.pallas_call(kernel, name='rechunk', out_shape=jax.ShapeDtypeStruct((Z,...  146 us

profile of v4, /device:TPU:1, one launch (start us, length us, event | category | flops | bytes accessed | tf_op | source)
XLA Modules:
  0.0 148.6 jit_solution(2100117543537102399)
XLA Ops:
  0.0 145.9 %rechunk.1 = f32[8,8,6,32,128]{4,3,2,1,0:T(8,128)S(1)} custom-call(f32[6,128,2048]{2,1,0:T(8,128)} %bitcast.3), custom_call_target="tpu_custom_call" | custom-call | tf_op jit(solution)/shard_map/rechunk/pallas_call | solution.py:196
  145.9 2.7 %copy.3 = f32[384,32,128]{2,1,0:T(8,128)} copy(f32[384,32,128]{2,1,0:T(8,128)S(1)} %bitcast.2) | data formatting | bytes 12582912

commit v5 on v4

--- a/solution.py
+++ b/solution.py
@@ -128,7 +128,7 @@
         if i == 3:
             pl.semaphore_wait(seen.at[1], 1)
             tell(seen.at[3], space=up)
-        send(first.at[i, :, pl.ds(within, COLS), :], out_ref.at[z, yc], zs_sem, early_sem.at[i], space=along_z(i))
+        send(first.at[i, :, pl.ds(within, COLS), :], out_ref.at[z, yc], zs_sem, early_sem, space=along_z(i))
 
     pl.semaphore_wait(seen.at[2], 1)
     tell(seen.at[4], space=down)
@@ -154,7 +154,7 @@
                 late[i, 0:ROWS] = jnp.where(half == 0, total[:, :LANES], total[:, LANES:])
             totals(i)
             if i < EARLY:
-                send(late.at[i], late_in.at[i], ls_sem, lr_sem.at[i], space=along_z(i))
+                send(late.at[i], late_in.at[i], ls_sem, lr_sem, space=along_z(i))
             elif HOPS[i]:
                 send(stage.at[yc, i], out_ref.at[z, yc], zs_sem, direct_sem, space=along_z(i))
             else:
@@ -175,9 +175,9 @@
                 if HOPS[i]:
                     send(relay.at[j, i], out_ref.at[z, source[j]], zs_sem, onward_sem, space=along_z(i))
 
+    arrived(stage.at[0, 0:EARLY], early_sem)
+    arrived(late_in, lr_sem)
     for i in range(EARLY):
-        arrived(stage.at[0, 0], early_sem.at[i])
-        arrived(late_in.at[i], lr_sem.at[i])
         column[i] = late_in[i].T
         origin = lax.rem(z + Z - HOPS[i], Z)
         for r in range(ROWS):
@@ -217,11 +217,11 @@
             pltpu.SemaphoreType.DMA((FINE, S)),
             pltpu.SemaphoreType.DMA((len(WAVES) - FINE,)),
             pltpu.SemaphoreType.DMA,
-            pltpu.SemaphoreType.DMA((EARLY,)),
-            pltpu.SemaphoreType.DMA,
-            pltpu.SemaphoreType.DMA,
-            pltpu.SemaphoreType.DMA,
-            pltpu.SemaphoreType.DMA((EARLY,)),
+            pltpu.SemaphoreType.DMA,
+            pltpu.SemaphoreType.DMA,
+            pltpu.SemaphoreType.DMA,
+            pltpu.SemaphoreType.DMA,
+            pltpu.SemaphoreType.DMA,
             pltpu.SemaphoreType.REGULAR((5,)),
             pltpu.SemaphoreType.REGULAR,
             pltpu.SemaphoreType.REGULAR,

time: 149 us -> 149 us (level)
  no operation moved by 1% of the time
where the time goes in v5:
time: 149 us
  Pallas kernels  146 us (98%)
  local copies, waits for them, and re-layouts  2.71 us (2%)
    pallas_call x1, Pallas kernels, per_device(): pl.pallas_call(kernel, name='rechunk', out_shape=jax.ShapeDtypeStruct((Z,...  146 us

profile of v5, /device:TPU:1, one launch (start us, length us, event | category | flops | bytes accessed | tf_op | source)
XLA Modules:
  0.0 148.6 jit_solution(15383831423877042753)
XLA Ops:
  0.0 145.8 %rechunk.1 = f32[8,8,6,32,128]{4,3,2,1,0:T(8,128)S(1)} custom-call(f32[6,128,2048]{2,1,0:T(8,128)} %bitcast.3), custom_call_target="tpu_custom_call" | custom-call | tf_op jit(solution)/shard_map/rechunk/pallas_call | solution.py:196
  145.8 2.7 %copy.3 = f32[384,32,128]{2,1,0:T(8,128)} copy(f32[384,32,128]{2,1,0:T(8,128)S(1)} %bitcast.2) | data formatting | bytes 12582912
